TPU v7x, 32 devices: a whole 2x2x4 slice. The times are simulated.
32 devices in a mesh: lat: 8 (over y, x, core), lon: 4 (over z).
Axes of the slice: x: 2, y: 2, z: 4, core: 2. Of those that a mesh axis runs over, the one named last changes fastest.
Arguments:
- pressure: float32 [256, 128, 128], P('lat', 'lon'), may hold values from 0.2 to 1.8
- earlier: float32 [256, 128, 128], P('lat', 'lon'), may hold values from 0.2 to 1.8
- speed_square: float32 [256, 128, 128], P('lat', 'lon'), may hold values from 0.05 to 0.4
Outputs:
- potential: float32 [256, 128, 128], P('lat', 'lon')
- pressure_end: float32 [256, 128, 128], P('lat', 'lon')
All inputs are finite; a program needn't handle non-finite values.
Results may differ from a plain program's by a relative error of at most 0.00002.
Values sent between devices are 32-bit elements; how exact they have to be, the bound alone decides.
A program may use at most 64 MiB of HBM per device.

v0:
```python
import jax
import jax.numpy as jnp
from jax import lax
from jax.sharding import PartitionSpec as P

STEPS = 4


def padded_2(block, sides, width):
    for axis, dim in sides:
        count = lax.axis_size(axis)
        forward = [(i, i + 1) for i in range(count - 1)]
        backward = [(target, source) for source, target in forward]
        low = lax.ppermute(
            lax.slice_in_dim(block, block.shape[dim] - width, None, axis=dim), axis, forward
        )
        high = lax.ppermute(lax.slice_in_dim(block, 0, width, axis=dim), axis, backward)
        block = jnp.concatenate([low, block, high], axis=dim)
    return block


def prefix(part, axis, combine, identity):
    place = lax.axis_index(axis)
    gathered = lax.all_gather(part, axis)
    state = jnp.zeros_like(part) + jnp.asarray(identity, part.dtype)

    def one(lap, state):
        return combine(state, lax.dynamic_index_in_dim(gathered, lap, 0, False))

    return lax.fori_loop(0, place, one, state)


def strip_edges(values, dims):
    for dim in dims:
        values = lax.slice_in_dim(values, 1, values.shape[dim] - 1, axis=dim)
    return values


def neighbour(values, dim, start, dims):
    others = [other for other in dims if other != dim]
    values = strip_edges(values, others)
    return lax.slice_in_dim(values, start, start + values.shape[dim] - 2, axis=dim)


def one_step(padded, before, speed_square):
    middle = strip_edges(padded, (0, 1))
    lower = [neighbour(padded, dim, 0, (0, 1)) for dim in (0, 1)]
    upper = [neighbour(padded, dim, 2, (0, 1)) for dim in (0, 1)]
    spread = lower[0] + upper[0] + lower[1] + upper[1] - 4.0 * middle
    return 2.0 * middle - before + speed_square * spread


def on_device(pressure, earlier, speed_square):
    padded = padded_2(pressure, (("lat", 0), ("lon", 1)), STEPS)
    wide_parts = padded_2(
        jnp.concatenate([earlier, speed_square], axis=2), (("lat", 0), ("lon", 1)), STEPS - 1
    )
    wide_earlier, wide_speed_square = jnp.split(wide_parts, 2, axis=2)
    for step in range(STEPS):
        later = one_step(padded, wide_earlier, wide_speed_square)
        values = later
        margin = STEPS - 1 - step
        place = lax.axis_index("lat") * pressure.shape[0] - margin + jnp.arange(values.shape[0])
        keep_cells = (place >= 0) & (place < pressure.shape[0] * lax.axis_size("lat"))
        values = jnp.where(keep_cells.reshape((-1,) + (1,) * 2), values, 0.0)
        place = lax.axis_index("lon") * pressure.shape[1] - margin + jnp.arange(values.shape[1])
        keep_cells = (place >= 0) & (place < pressure.shape[1] * lax.axis_size("lon"))
        values = jnp.where(keep_cells.reshape((-1,) + (1,) * 1), values, 0.0)
        later = values
        before = strip_edges(padded, (0, 1))
        if step < STEPS - 1:
            wide_earlier = strip_edges(before, (0, 1))
            wide_speed_square = strip_edges(wide_speed_square, (0, 1))
        padded = later
    pressure = padded
    here = jnp.cumsum(pressure, axis=0)
    total = lax.slice_in_dim(here, here.shape[0] - 1, here.shape[0], axis=0)

    def add_pair(earlier_total, later_total):
        return earlier_total + later_total

    below = prefix(total, "lat", add_pair, jnp.zeros_like(total))
    potential = (here + below) / (pressure.shape[0] * lax.axis_size("lat"))
    return (potential, pressure)


def solution(mesh):
    in_specs = (P("lat", "lon", None), P("lat", "lon", None), P("lat", "lon", None))
    out_specs = (P("lat", "lon", None), P("lat", "lon", None))
    return jax.shard_map(
        on_device, mesh=mesh, in_specs=in_specs, out_specs=out_specs, check_vma=False
    )
```

profile of v0, /device:TPU:0, one launch (start us, length us, event | category | flops | bytes accessed | tf_op | source)
XLA Modules:
  0.0 50.5 jit_solution(10274606888290544367)
XLA Ops:
  0.6 0.0 copy-start.2
  0.6 1.1 %constant_dynamic-update-slice_fusion.4 = f32[32,32,256]{2,1,0:T(8,128)S(1)} fusion(f32[32,32,128]{2,1,0:T(8,128)} %param.6), kind=kLoop, calls=%fused_computation.47 | loop fusion | bytes 1048576
  1.8 1.1 %constant_dynamic-update-slice_fusion.3 = f32[32,32,256]{2,1,0:T(8,128)S(1)} fusion(f32[32,32,256]{2,1,0:T(8,128)S(1)} %constant_dynamic-update-slice_fusion.4, f32[32,32,128]{2,1,0:T(8,128)} %param.7), kind=kLoop, calls=%fused_computation.46 | loop fusion | bytes 1048576 | tf_op jit(solution)/shard_map/concatenate | solution.py:56
  2.9 2.4 %collective-permute-start.4 = (f32[3,32,256]{2,1,0:T(8,128)S(1)}, f32[3,32,256]{2,1,0:T(8,128)S(1)}, u32[]{:S(2)}, u32[]{:S(2)}) collective-permute-start(f32[3,32,256]{2,1,0:T(8,128)S(1)} %get-tuple-element.44), channel_id=1, source_target_pairs={{0,4},{4,8},{8,12},{12,16},{16,20},{20,24},{24,28},{1,5},{5,9},{9,... | collective-permute-start | bytes 294920 | tf_op jit(solution)/shard_map/ppermute | solution.py:14
  5.3 1.3 %collective-permute-start.5 = (f32[3,32,256]{2,1,0:T(8,128)S(1)}, f32[3,32,256]{2,1,0:T(8,128)S(1)}, u32[]{:S(2)}, u32[]{:S(2)}) collective-permute-start(f32[3,32,256]{2,1,0:T(8,128)S(1)} %get-tuple-element.45), channel_id=1, source_target_pairs={{4,0},{8,4},{12,8},{16,12},{20,16},{24,20},{28,24},{5,1},{9,5},{13... | collective-permute-start | bytes 294920 | tf_op jit(solution)/shard_map/ppermute | solution.py:17
  6.6 5.1 %collective-permute-start = (f32[4,32,128]{2,1,0:T(8,128)S(1)}, f32[4,32,128]{2,1,0:T(8,128)S(1)}, u32[]{:S(2)}, u32[]{:S(2)}) collective-permute-start(f32[4,32,128]{2,1,0:T(8,128)S(1)} %get-tuple-element.49), channel_id=1, source_target_pairs={{0,4},{4,8},{8,12},{12,16},{16,20},{20,24},{24,28},{1,5},{5,9},{9,... | collective-permute-start | bytes 196616 | tf_op jit(solution)/shard_map/ppermute | solution.py:14
  11.8 1.3 %collective-permute-start.1 = (f32[4,32,128]{2,1,0:T(8,128)S(1)}, f32[4,32,128]{2,1,0:T(8,128)S(1)}, u32[]{:S(2)}, u32[]{:S(2)}) collective-permute-start(f32[4,32,128]{2,1,0:T(8,128)S(1)} %get-tuple-element.48), channel_id=1, source_target_pairs={{4,0},{8,4},{12,8},{16,12},{20,16},{24,20},{28,24},{5,1},{9,5},{13... | collective-permute-start | bytes 196616 | tf_op jit(solution)/shard_map/ppermute | solution.py:17
  13.1 0.0 collective-permute-done
  13.2 2.9 %collective-permute-done.1 = f32[4,32,128]{2,1,0:T(8,128)S(1)} collective-permute-done((f32[4,32,128]{2,1,0:T(8,128)S(1)}, f32[4,32,128]{2,1,0:T(8,128)S(1)}, u32[]{:S(2)}, u32[]{:S(2)}) %collective-permute-start.1) | collective-permute-done | bytes 65568 | tf_op jit(solution)/shard_map/ppermute | solution.py:17
  16.2 3.5 %collective-permute-start.2 = (f32[40,4,128]{2,1,0:T(4,128)S(1)}, f32[40,4,128]{2,1,0:T(4,128)S(1)}, u32[]{:S(2)}, u32[]{:S(2)}) collective-permute-start(f32[40,4,128]{2,1,0:T(4,128)S(1)} %get-tuple-element.46), channel_id=1, source_target_pairs={{0,1},{1,2},{2,3},{4,5},{5,6},{6,7},{8,9},{9,10},{10,11},{12,13},{... | collective-permute-start | bytes 245768 | tf_op jit(solution)/shard_map/ppermute | solution.py:14
  19.7 1.3 %collective-permute-start.3 = (f32[40,4,128]{2,1,0:T(4,128)S(1)}, f32[40,4,128]{2,1,0:T(4,128)S(1)}, u32[]{:S(2)}, u32[]{:S(2)}) collective-permute-start(f32[40,4,128]{2,1,0:T(4,128)S(1)} %get-tuple-element.47), channel_id=1, source_target_pairs={{1,0},{2,1},{3,2},{5,4},{6,5},{7,6},{9,8},{10,9},{11,10},{13,12},{... | collective-permute-start | bytes 245768 | tf_op jit(solution)/shard_map/ppermute | solution.py:17
  21.0 0.0 collective-permute-done.4
  21.0 0.0 collective-permute-done.5
  21.0 0.1 pad_maximum_fusion.4
  21.1 4.6 %collective-permute-start.6 = (f32[38,3,256]{2,1,0:T(4,128)S(1)}, f32[38,3,256]{2,1,0:T(4,128)S(1)}, u32[]{:S(2)}, u32[]{:S(2)}) collective-permute-start(f32[38,3,256]{2,1,0:T(4,128)S(1)} %get-tuple-element.42), channel_id=1, source_target_pairs={{0,1},{1,2},{2,3},{4,5},{5,6},{6,7},{8,9},{9,10},{10,11},{12,13},{... | collective-permute-start | bytes 350216 | tf_op jit(solution)/shard_map/ppermute | solution.py:14
  25.6 1.3 %collective-permute-start.7 = (f32[38,3,256]{2,1,0:T(4,128)S(1)}, f32[38,3,256]{2,1,0:T(4,128)S(1)}, u32[]{:S(2)}, u32[]{:S(2)}) collective-permute-start(f32[38,3,256]{2,1,0:T(4,128)S(1)} %get-tuple-element.43), channel_id=1, source_target_pairs={{1,0},{2,1},{3,2},{5,4},{6,5},{7,6},{9,8},{10,9},{11,10},{13,12},{... | collective-permute-start | bytes 350216 | tf_op jit(solution)/shard_map/ppermute | solution.py:17
  26.9 0.0 collective-permute-done.2
  26.9 0.0 collective-permute-done.3
  27.0 0.1 pad_maximum_fusion.1
  27.1 1.5 %collective-permute-done.6 = f32[38,3,256]{2,1,0:T(4,128)S(1)} collective-permute-done((f32[38,3,256]{2,1,0:T(4,128)S(1)}, f32[38,3,256]{2,1,0:T(4,128)S(1)}, u32[]{:S(2)}, u32[]{:S(2)}) %collective-permute-start.6) | collective-permute-done | bytes 116768 | tf_op jit(solution)/shard_map/ppermute | solution.py:14
  28.6 4.7 %collective-permute-done.7 = f32[38,3,256]{2,1,0:T(4,128)S(1)} collective-permute-done((f32[38,3,256]{2,1,0:T(4,128)S(1)}, f32[38,3,256]{2,1,0:T(4,128)S(1)}, u32[]{:S(2)}, u32[]{:S(2)}) %collective-permute-start.7) | collective-permute-done | bytes 116768 | tf_op jit(solution)/shard_map/ppermute | solution.py:17
  33.3 0.2 pad_maximum_fusion
  33.5 0.4 fusion.4
  33.9 0.5 %fusion.9 = f32[36,36,128]{2,1,0:T(8,128)S(1)} fusion(f32[38,38,128]{2,1,0:T(8,128)S(1)} %fusion.4, f32[38,38,256]{2,1,0:T(8,128)S(1)} %pad_maximum_fusion, f32[40,40,128]{2,1,0:T(8,128)S(1)} %pad_maximum_fusion.1, pred[36]{0:T(512)(128)(4,1)S(1)} %get-tuple-element.52, pred[36]{0:T(512)(128)(4,1)S(1)} %get-tuple-element.53), kind=kLoop, calls=%fused_computation.17 | loop fusion | flops 1824768 | bytes 5308488 | tf_op jit(solution)/shard_map/jit(_where)/select_n | solution.py:68
  34.5 0.0 copy-start
  34.5 0.5 fusion.14
  35.0 0.5 %copy-done = f32[32,32,128]{2,1,0:T(8,128)S(1)} copy-done((f32[32,32,128]{2,1,0:T(8,128)S(1)}, f32[32,32,128]{2,1,0:T(8,128)}, u32[]{:S(2)}) %copy-start) | copy-done | bytes 524312
  35.5 0.3 fusion.19
  35.8 0.0 copy-start.1
  35.9 2.0 %fusion.23 = f32[32,32,128]{2,1,0:T(8,128)S(1)} fusion(f32[32,32,128]{2,1,0:T(8,128)S(1)} %fusion.19), kind=kOutput, calls=%fused_computation.59 | output fusion | flops 4063232 | bytes 1048576 | tf_op jit(solution)/shard_map/jit(cumsum)/reduce_window_sum | solution.py:76
  37.9 11.8 %all-gather = f32[8,32,128]{2,1,0:T(8,128)S(1)} all-gather(f32[1,32,128]{2,1,0:T(8,128)S(1)} %slice.232), channel_id=2, replica_groups=mesh['lat'=8,'lon'=4] {'lat'}, dimensions={0}, use_global_device_ids=true | all-gather | bytes 147456 | tf_op jit(solution)/shard_map/all_gather | solution.py:24
  49.6 0.9 %add_multiply_fusion = f32[32,32,128]{2,1,0:T(8,128)} fusion(f32[32,32,128]{2,1,0:T(8,128)S(1)} %fusion.23, f32[32,128]{1,0:T(8,128)S(1)} %bitcast.9), kind=kLoop, calls=%fused_computation.39 | loop fusion | flops 262144 | bytes 1064960 | tf_op jit(solution)/shard_map/div | solution.py:83
  (15 shorter events, 0.2 us)
Async XLA Ops:
  0.6 6.0 %copy-start.2 = (f32[32,32,128]{2,1,0:T(8,128)S(1)}, f32[32,32,128]{2,1,0:T(8,128)}, u32[]{:S(2)}) copy-start(f32[32,32,128]{2,1,0:T(8,128)} %param.5) | copy-start | bytes 1572868
  2.9 18.1 %collective-permute-start.4 = (f32[3,32,256]{2,1,0:T(8,128)S(1)}, f32[3,32,256]{2,1,0:T(8,128)S(1)}, u32[]{:S(2)}, u32[]{:S(2)}) collective-permute-start(f32[3,32,256]{2,1,0:T(8,128)S(1)} %get-tuple-element.44), channel_id=1, source_target_pairs={{0,4},{4,8},{8,12},{12,16},{16,20},{20,24},{24,28},{1,5},{5,9},{9,... | collective-permute-start | bytes 294920 | tf_op jit(solution)/shard_map/ppermute | solution.py:14
  5.3 15.7 %collective-permute-start.5 = (f32[3,32,256]{2,1,0:T(8,128)S(1)}, f32[3,32,256]{2,1,0:T(8,128)S(1)}, u32[]{:S(2)}, u32[]{:S(2)}) collective-permute-start(f32[3,32,256]{2,1,0:T(8,128)S(1)} %get-tuple-element.45), channel_id=1, source_target_pairs={{4,0},{8,4},{12,8},{16,12},{20,16},{24,20},{28,24},{5,1},{9,5},{13... | collective-permute-start | bytes 294920 | tf_op jit(solution)/shard_map/ppermute | solution.py:17
  6.6 6.5 %collective-permute-start = (f32[4,32,128]{2,1,0:T(8,128)S(1)}, f32[4,32,128]{2,1,0:T(8,128)S(1)}, u32[]{:S(2)}, u32[]{:S(2)}) collective-permute-start(f32[4,32,128]{2,1,0:T(8,128)S(1)} %get-tuple-element.49), channel_id=1, source_target_pairs={{0,4},{4,8},{8,12},{12,16},{16,20},{20,24},{24,28},{1,5},{5,9},{9,... | collective-permute-start | bytes 196616 | tf_op jit(solution)/shard_map/ppermute | solution.py:14
  11.8 4.4 %collective-permute-start.1 = (f32[4,32,128]{2,1,0:T(8,128)S(1)}, f32[4,32,128]{2,1,0:T(8,128)S(1)}, u32[]{:S(2)}, u32[]{:S(2)}) collective-permute-start(f32[4,32,128]{2,1,0:T(8,128)S(1)} %get-tuple-element.48), channel_id=1, source_target_pairs={{4,0},{8,4},{12,8},{16,12},{20,16},{24,20},{28,24},{5,1},{9,5},{13... | collective-permute-start | bytes 196616 | tf_op jit(solution)/shard_map/ppermute | solution.py:17
  16.2 10.7 %collective-permute-start.2 = (f32[40,4,128]{2,1,0:T(4,128)S(1)}, f32[40,4,128]{2,1,0:T(4,128)S(1)}, u32[]{:S(2)}, u32[]{:S(2)}) collective-permute-start(f32[40,4,128]{2,1,0:T(4,128)S(1)} %get-tuple-element.46), channel_id=1, source_target_pairs={{0,1},{1,2},{2,3},{4,5},{5,6},{6,7},{8,9},{9,10},{10,11},{12,13},{... | collective-permute-start | bytes 245768 | tf_op jit(solution)/shard_map/ppermute | solution.py:14
  19.7 7.3 %collective-permute-start.3 = (f32[40,4,128]{2,1,0:T(4,128)S(1)}, f32[40,4,128]{2,1,0:T(4,128)S(1)}, u32[]{:S(2)}, u32[]{:S(2)}) collective-permute-start(f32[40,4,128]{2,1,0:T(4,128)S(1)} %get-tuple-element.47), channel_id=1, source_target_pairs={{1,0},{2,1},{3,2},{5,4},{6,5},{7,6},{9,8},{10,9},{11,10},{13,12},{... | collective-permute-start | bytes 245768 | tf_op jit(solution)/shard_map/ppermute | solution.py:17
  21.1 7.5 %collective-permute-start.6 = (f32[38,3,256]{2,1,0:T(4,128)S(1)}, f32[38,3,256]{2,1,0:T(4,128)S(1)}, u32[]{:S(2)}, u32[]{:S(2)}) collective-permute-start(f32[38,3,256]{2,1,0:T(4,128)S(1)} %get-tuple-element.42), channel_id=1, source_target_pairs={{0,1},{1,2},{2,3},{4,5},{5,6},{6,7},{8,9},{9,10},{10,11},{12,13},{... | collective-permute-start | bytes 350216 | tf_op jit(solution)/shard_map/ppermute | solution.py:14
  25.6 7.7 %collective-permute-start.7 = (f32[38,3,256]{2,1,0:T(4,128)S(1)}, f32[38,3,256]{2,1,0:T(4,128)S(1)}, u32[]{:S(2)}, u32[]{:S(2)}) collective-permute-start(f32[38,3,256]{2,1,0:T(4,128)S(1)} %get-tuple-element.43), channel_id=1, source_target_pairs={{1,0},{2,1},{3,2},{5,4},{6,5},{7,6},{9,8},{10,9},{11,10},{13,12},{... | collective-permute-start | bytes 350216 | tf_op jit(solution)/shard_map/ppermute | solution.py:17
  34.5 1.0 %copy-start = (f32[32,32,128]{2,1,0:T(8,128)S(1)}, f32[32,32,128]{2,1,0:T(8,128)}, u32[]{:S(2)}) copy-start(f32[32,32,128]{2,1,0:T(8,128)} %param.7) | copy-start | bytes 1572868
  35.8 14.7 %copy-start.1 = (f32[32,32,128]{2,1,0:T(8,128)}, f32[32,32,128]{2,1,0:T(8,128)S(1)}, u32[]{:S(2)}) copy-start(f32[32,32,128]{2,1,0:T(8,128)S(1)} %fusion.19) | copy-start | bytes 1572868
where the time goes:
time: 50.9 us; the launch traced here: 50.5 us
  starting transfers between devices  20.7 us (41%)
  blocking collectives  11.8 us (23%)
  waiting for transfers between devices  9.18 us (18%)
  other arithmetic  5.02 us (10%)
  local copies, waits for them, and re-layouts  2.88 us (6%)
  between operations  0.9 us (2%)
    ppermute x4, starting transfers between devices, padded_2(): lax.ppermute(lax.slice_in_dim(block, block.shape[dim] - width, None, axis...  15.6 us
    all_gather x1, blocking collectives, prefix(): gathered = lax.all_gather(part, axis)  11.8 us
    ppermute x4, waiting for transfers between devices, padded_2(): lax.ppermute(lax.slice_in_dim(block, 0, width, axis=dim), axis, backward)  7.63 us
    ppermute x4, starting transfers between devices, padded_2(): lax.ppermute(lax.slice_in_dim(block, 0, width, axis=dim), axis, backward)  5.17 us
    another operation x1, other arithmetic, on_device(): here = jnp.cumsum(pressure, axis=0)  2 us
    select_n x4, other arithmetic, on_device(): values = jnp.where(keep_cells.reshape((-1,) + (1,) * 1), values, 0.0)  1.75 us
    unnamed x9, local copies, waits for them, and re-layouts  1.73 us
    ppermute x4, waiting for transfers between devices, padded_2(): lax.ppermute(lax.slice_in_dim(block, block.shape[dim] - width, None, axis...  1.56 us
  transfers between devices with their start and end apart: 8, of which 3 were waited for; matrix products, arithmetic and copies ran while one was open for 1% of the time, Pallas kernels for 0%

commit v1 on v0

v1 whole, which is shorter than its diff:
```python
import functools

import jax
import jax.numpy as jnp
from jax import lax
from jax.experimental import pallas as pl
from jax.experimental.pallas import tpu as pltpu
from jax.sharding import PartitionSpec as P

STEPS = 4
PAD = 8
MESH = pl.DeviceIdType.MESH


def corner_cells():
    cells = [(0, i, j) for i in range(STEPS - 1) for j in range(STEPS - 1 - i)]
    for array in (1, 2):
        cells += [(array, i, j) for i in range(STEPS - 2) for j in range(STEPS - 2 - i)]
    return cells


def kernel(
    n_lat, n_lon, p_in, e_in, c_in, pot_out, end_out,
    p, e, c, lon_send, lon_recv, corner_send, corner_recv, here, totals, below,
    load_sem, store_sem, lat_sems, lon_sems, corner_sems, total_send_sem, total_recv_sem,
):
    rows, cols = p_in.shape[0], p_in.shape[1]
    fields = (p, e, c)
    depth = (STEPS, STEPS - 1, STEPS - 1)
    top, left = STEPS, PAD
    bottom, right = top + rows, left + cols
    me_lat, me_lon = lax.axis_index("lat"), lax.axis_index("lon")
    has_lat = (me_lat > 0, me_lat < n_lat - 1)
    has_lon = (me_lon > 0, me_lon < n_lon - 1)
    step_of = (-1, 1)

    loads = []
    for k, (src, dst) in enumerate(zip((p_in, e_in, c_in), fields)):
        copy = pltpu.make_async_copy(src, dst.at[top:bottom, left:right], load_sem.at[k])
        copy.start()
        loads.append(copy)

    barrier = pltpu.get_barrier_semaphore()

    def greet(lat, lon):
        pl.semaphore_signal(
            barrier, inc=1, device_id={"lat": lat, "lon": lon}, device_id_type=MESH
        )

    for a in range(2):
        for b in range(2):
            @pl.when(has_lat[a] & has_lon[b])
            def _():
                greet(me_lat + step_of[a], me_lon + step_of[b])
    for b in range(2):
        @pl.when(has_lon[b])
        def _():
            greet(me_lat, me_lon + step_of[b])
    for j in range(n_lat):
        @pl.when(me_lat != j)
        def _():
            greet(j, me_lon)

    zero = jnp.int32(0)
    one = jnp.int32(1)
    count_lat = sum(jnp.where(h, one, zero) for h in has_lat)
    count_lon = sum(jnp.where(h, one, zero) for h in has_lon)
    peers = n_lat - 1 + count_lon + count_lon * count_lat

    for a in range(2):
        @pl.when(jnp.logical_not(has_lat[a]))
        def _():
            for f in fields:
                start = 0 if a == 0 else bottom
                f[start:start + STEPS] = jnp.zeros((STEPS,) + f.shape[1:], f.dtype)
    for b in range(2):
        @pl.when(jnp.logical_not(has_lon[b]))
        def _():
            for f in fields:
                start = 0 if b == 0 else right
                f[:, start:start + PAD] = jnp.zeros((f.shape[0], PAD, f.shape[2]), f.dtype)

    for copy in loads:
        copy.wait()

    for b in range(2):
        @pl.when(has_lon[b])
        def _():
            base = 0
            for f, d in zip(fields, depth):
                start = left if b == 0 else right - d
                for r in range(rows):
                    lon_send[b, base + r * d:base + (r + 1) * d] = f[top + r, start:start + d]
                base += rows * d
    cells = corner_cells()
    for a in range(2):
        for b in range(2):
            @pl.when(has_lat[a] & has_lon[b])
            def _():
                for k, (which, i, j) in enumerate(cells):
                    r = top + i if a == 0 else bottom - 1 - i
                    s = left + j if b == 0 else right - 1 - j
                    corner_send[2 * a + b, k:k + 1] = fields[which][r, s:s + 1]

    pl.semaphore_wait(barrier, peers)

    def corner_copy(a, b):
        return pltpu.make_async_remote_copy(
            src_ref=corner_send.at[2 * a + b],
            dst_ref=corner_recv.at[2 * (1 - a) + 1 - b],
            send_sem=corner_sems.at[0, 2 * a + b],
            recv_sem=corner_sems.at[1, 2 * (1 - a) + 1 - b],
            device_id={"lat": me_lat + step_of[a], "lon": me_lon + step_of[b]},
            device_id_type=MESH,
        )

    def lon_copy(b):
        return pltpu.make_async_remote_copy(
            src_ref=lon_send.at[b],
            dst_ref=lon_recv.at[1 - b],
            send_sem=lon_sems.at[0, b],
            recv_sem=lon_sems.at[1, 1 - b],
            device_id={"lat": me_lat, "lon": me_lon + step_of[b]},
            device_id_type=MESH,
        )

    def lat_copy(a, k):
        f, d = fields[k], depth[k]
        src = top if a == 0 else bottom - d
        dst = bottom if a == 0 else top - d
        return pltpu.make_async_remote_copy(
            src_ref=f.at[src:src + d, left:right],
            dst_ref=f.at[dst:dst + d, left:right],
            send_sem=lat_sems.at[0, a, k],
            recv_sem=lat_sems.at[1, 1 - a, k],
            device_id={"lat": me_lat + step_of[a], "lon": me_lon},
            device_id_type=MESH,
        )

    for a in range(2):
        for b in range(2):
            @pl.when(has_lat[a] & has_lon[b])
            def _():
                corner_copy(a, b).start()
    for b in range(2):
        @pl.when(has_lon[b])
        def _():
            lon_copy(b).start()
    for a in range(2):
        @pl.when(has_lat[a])
        def _():
            for k in range(3):
                lat_copy(a, k).start()

    for a in range(2):
        for b in range(2):
            @pl.when(has_lat[a] & has_lon[b])
            def _():
                corner_copy(1 - a, 1 - b).wait_recv()
                corner_copy(a, b).wait_send()
                for k, (which, i, j) in enumerate(cells):
                    r = top - 1 - i if a == 0 else bottom + i
                    s = left - 1 - j if b == 0 else right + j
                    fields[which][r, s:s + 1] = corner_recv[2 * a + b, k:k + 1]
    for b in range(2):
        @pl.when(has_lon[b])
        def _():
            lon_copy(1 - b).wait_recv()
            lon_copy(b).wait_send()
            base = 0
            for f, d in zip(fields, depth):
                start = left - d if b == 0 else right
                for r in range(rows):
                    f[top + r, start:start + d] = lon_recv[b, base + r * d:base + (r + 1) * d]
                base += rows * d
    for a in range(2):
        @pl.when(has_lat[a])
        def _():
            for k in range(3):
                lat_copy(1 - a, k).wait_recv()
                lat_copy(a, k).wait_send()

    now, old = p, e
    for step in range(STEPS):
        margin = STEPS - 1 - step
        lo, hi = left - margin, right + margin
        last = step == STEPS - 1

        def one_row(r, total, now=now, old=old, lo=lo, hi=hi, last=last):
            middle = now[r, lo:hi]
            spread = (
                now[r - 1, lo:hi] + now[r + 1, lo:hi]
                + now[r, lo - 1:hi - 1] + now[r, lo + 1:hi + 1] - 4.0 * middle
            )
            later = 2.0 * middle - old[r, lo:hi] + c[r, lo:hi] * spread
            old[r, lo:hi] = later
            if last:
                total = total + later
                here[r - top] = total
            return total

        start = jnp.zeros((cols, p.shape[2]), p.dtype) if last else 0
        total = lax.fori_loop(top - margin, bottom + margin, one_row, start, unroll=2)
        now, old = old, now
    below[...] = total

    def total_copy(j):
        return pltpu.make_async_remote_copy(
            src_ref=below,
            dst_ref=totals.at[me_lat],
            send_sem=total_send_sem.at[j],
            recv_sem=total_recv_sem.at[me_lat],
            device_id={"lat": j, "lon": me_lon},
            device_id_type=MESH,
        )

    def total_arrival(j):
        return pltpu.make_async_remote_copy(
            src_ref=below,
            dst_ref=totals.at[j],
            send_sem=total_send_sem.at[j],
            recv_sem=total_recv_sem.at[j],
            device_id={"lat": j, "lon": me_lon},
            device_id_type=MESH,
        )

    for j in reversed(range(1, n_lat)):
        @pl.when(me_lat < j)
        def _():
            total_copy(j).start()
    end_copy = pltpu.make_async_copy(
        now.at[top:bottom, left:right], end_out, store_sem.at[0]
    )
    end_copy.start()

    def arrive(j, acc):
        total_arrival(j).wait_recv()
        return acc + totals[j]

    before = lax.fori_loop(0, me_lat, arrive, jnp.zeros((cols, p.shape[2]), p.dtype))
    scale = 1.0 / (rows * n_lat)

    def finish(r, carry):
        here[r] = (here[r] + before) * scale
        return carry

    lax.fori_loop(0, rows, finish, 0, unroll=4)
    pot_copy = pltpu.make_async_copy(here, pot_out, store_sem.at[1])
    pot_copy.start()
    for j in range(1, n_lat):
        @pl.when(me_lat < j)
        def _():
            total_copy(j).wait_send()
    end_copy.wait()
    pot_copy.wait()


def on_device(n_lat, n_lon, pressure, earlier, speed_square):
    rows, cols, members = pressure.shape
    packed = rows * (3 * STEPS - 2)
    corner_rows = -(-len(corner_cells()) // 8) * 8
    f32 = jnp.float32
    wide = pltpu.VMEM((rows + 2 * STEPS, cols + 2 * PAD, members), f32)
    any_space = pl.BlockSpec(memory_space=pl.ANY)
    dma = pltpu.SemaphoreType.DMA
    return pl.pallas_call(
        functools.partial(kernel, n_lat, n_lon),
        out_shape=[jax.ShapeDtypeStruct(pressure.shape, f32)] * 2,
        in_specs=[any_space] * 3,
        out_specs=[any_space] * 2,
        scratch_shapes=[
            wide, wide, wide,
            pltpu.VMEM((2, packed, members), f32),
            pltpu.VMEM((2, packed, members), f32),
            pltpu.VMEM((4, corner_rows, members), f32),
            pltpu.VMEM((4, corner_rows, members), f32),
            pltpu.VMEM((rows, cols, members), f32),
            pltpu.VMEM((n_lat, cols, members), f32),
            pltpu.VMEM((cols, members), f32),
            dma((3,)), dma((2,)), dma((2, 2, 3)), dma((2, 2)), dma((2, 4)),
            dma((n_lat,)), dma((n_lat,)),
        ],
        compiler_params=pltpu.CompilerParams(collective_id=0, has_side_effects=True),
        name="waves",
    )(pressure, earlier, speed_square)


def solution(mesh):
    spec = P("lat", "lon", None)
    body = functools.partial(on_device, mesh.shape["lat"], mesh.shape["lon"])
    return jax.shard_map(
        body, mesh=mesh, in_specs=(spec,) * 3, out_specs=(spec,) * 2, check_vma=False
    )
```

time: 50.9 us -> 18.2 us (0.36)
  the two profiles are of different devices: /device:TPU:0 before, /device:TPU:13 now
where the time goes in v1:
time: 18.2 us; the launch traced here: 18 us
  Pallas kernels  14.6 us (80%)
  local copies, waits for them, and re-layouts  2.72 us (15%)
  between operations  0.65 us (4%)
    pallas_call x1, Pallas kernels, on_device(): pl.pallas_call(functools.partial(kernel, n_lat, n_lon), out_shape=[jax.Sh...  14.6 us
    unnamed x4, local copies, waits for them, and re-layouts  2.72 us

profile of v1, /device:TPU:13, one launch (start us, length us, event | category | flops | bytes accessed | tf_op | source)
XLA Modules:
  0.0 18.0 jit_solution(5326926139045499497)
XLA Ops:
  0.6 14.6 %waves.1 = (f32[32,32,128]{2,1,0:T(8,128)}, f32[32,32,128]{2,1,0:T(8,128)}) custom-call(f32[32,32,128]{2,1,0:T(8,128)} %p_in.1, f32[32,32,128]{2,1,0:T(8,128)} %e_in.1, f32[32,32,128]{2,1,0:T(8,128)} %c_in.1), custom_call_target="tpu_custom_call" | custom-call | tf_op jit(solution)/shard_map/waves/pallas_call | solution.py:266
  15.3 0.0 copy-start
  15.3 1.9 %copy.7 = f32[32,32,128]{2,1,0:T(8,128)} copy(f32[32,32,128]{2,1,0:T(8,128)} %get-tuple-element.4) | data formatting | bytes 1048576
  17.2 0.0 copy-done
  17.2 0.8 %copy.8 = f32[32,32,128]{2,1,0:T(8,128)} copy(f32[32,32,128]{2,1,0:T(8,128)S(1)} %copy-done) | data formatting | bytes 1048576
Async XLA Ops:
  15.3 1.9 %copy-start = (f32[32,32,128]{2,1,0:T(8,128)S(1)}, f32[32,32,128]{2,1,0:T(8,128)}, u32[]{:S(2)}) copy-start(f32[32,32,128]{2,1,0:T(8,128)} %get-tuple-element.5) | copy-start | bytes 1572868

commit v2 on v1

--- a/solution.py
+++ b/solution.py
@@ -20,9 +20,9 @@
 
 
 def kernel(
-    n_lat, n_lon, p_in, e_in, c_in, pot_out, end_out,
-    p, e, c, lon_send, lon_recv, corner_send, corner_recv, here, totals, below,
-    load_sem, store_sem, lat_sems, lon_sems, corner_sems, total_send_sem, total_recv_sem,
+    n_lat, n_lon, p_in, e_in, c_in, here, end, before,
+    p, e, c, lon_send, lon_recv, corner_send, corner_recv, totals, below,
+    load_sem, lat_sems, lon_sems, corner_sems, total_send_sem, total_recv_sem,
 ):
     rows, cols = p_in.shape[0], p_in.shape[1]
     fields = (p, e, c)
@@ -193,8 +193,10 @@
                 + now[r, lo - 1:hi - 1] + now[r, lo + 1:hi + 1] - 4.0 * middle
             )
             later = 2.0 * middle - old[r, lo:hi] + c[r, lo:hi] * spread
-            old[r, lo:hi] = later
-            if last:
+            if not last:
+                old[r, lo:hi] = later
+            else:
+                end[r - top] = later
                 total = total + later
                 here[r - top] = total
             return total
@@ -228,31 +230,33 @@
         @pl.when(me_lat < j)
         def _():
             total_copy(j).start()
-    end_copy = pltpu.make_async_copy(
-        now.at[top:bottom, left:right], end_out, store_sem.at[0]
-    )
-    end_copy.start()
-
     def arrive(j, acc):
         total_arrival(j).wait_recv()
         return acc + totals[j]
 
-    before = lax.fori_loop(0, me_lat, arrive, jnp.zeros((cols, p.shape[2]), p.dtype))
-    scale = 1.0 / (rows * n_lat)
-
-    def finish(r, carry):
-        here[r] = (here[r] + before) * scale
-        return carry
-
-    lax.fori_loop(0, rows, finish, 0, unroll=4)
-    pot_copy = pltpu.make_async_copy(here, pot_out, store_sem.at[1])
-    pot_copy.start()
+    before[...] = lax.fori_loop(0, me_lat, arrive, jnp.zeros((cols, p.shape[2]), p.dtype))
     for j in range(1, n_lat):
         @pl.when(me_lat < j)
         def _():
             total_copy(j).wait_send()
+
+
+def finish(scale, here, end, before, pot_out, end_out, pot, sems):
+    rows = here.shape[0]
+    end_copy = pltpu.make_async_copy(end, end_out, sems.at[0])
+    end_copy.start()
+    half = rows // 2
+    copies = []
+    for part in range(2):
+        for r in range(part * half, (part + 1) * half):
+            pot[r] = (here[r] + before[...]) * scale
+        span = pl.ds(part * half, half)
+        copy = pltpu.make_async_copy(pot.at[span], pot_out.at[span], sems.at[1 + part])
+        copy.start()
+        copies.append(copy)
+    for copy in copies:
+        copy.wait()
     end_copy.wait()
-    pot_copy.wait()
 
 
 def on_device(n_lat, n_lon, pressure, earlier, speed_square):
@@ -263,26 +267,36 @@
     wide = pltpu.VMEM((rows + 2 * STEPS, cols + 2 * PAD, members), f32)
     any_space = pl.BlockSpec(memory_space=pl.ANY)
     dma = pltpu.SemaphoreType.DMA
-    return pl.pallas_call(
+    vmem = pltpu.MemorySpace.VMEM
+    here, end, before = pl.pallas_call(
         functools.partial(kernel, n_lat, n_lon),
-        out_shape=[jax.ShapeDtypeStruct(pressure.shape, f32)] * 2,
+        out_shape=[
+            vmem(pressure.shape, f32), vmem(pressure.shape, f32), vmem((cols, members), f32)
+        ],
         in_specs=[any_space] * 3,
-        out_specs=[any_space] * 2,
+        out_specs=[pl.BlockSpec(memory_space=vmem)] * 3,
         scratch_shapes=[
             wide, wide, wide,
             pltpu.VMEM((2, packed, members), f32),
             pltpu.VMEM((2, packed, members), f32),
             pltpu.VMEM((4, corner_rows, members), f32),
             pltpu.VMEM((4, corner_rows, members), f32),
-            pltpu.VMEM((rows, cols, members), f32),
             pltpu.VMEM((n_lat, cols, members), f32),
             pltpu.VMEM((cols, members), f32),
-            dma((3,)), dma((2,)), dma((2, 2, 3)), dma((2, 2)), dma((2, 4)),
+            dma((3,)), dma((2, 2, 3)), dma((2, 2)), dma((2, 4)),
             dma((n_lat,)), dma((n_lat,)),
         ],
         compiler_params=pltpu.CompilerParams(collective_id=0, has_side_effects=True),
         name="waves",
     )(pressure, earlier, speed_square)
+    return pl.pallas_call(
+        functools.partial(finish, 1.0 / (rows * n_lat)),
+        out_shape=[jax.ShapeDtypeStruct(pressure.shape, f32)] * 2,
+        in_specs=[pl.BlockSpec(memory_space=vmem)] * 3,
+        out_specs=[any_space] * 2,
+        scratch_shapes=[pltpu.VMEM(pressure.shape, f32), dma((3,))],
+        name="finish",
+    )(*(pltpu.with_memory_space_constraint(x, vmem) for x in (here, end, before)))
 
 
 def solution(mesh):

time: 18.2 us -> 15.9 us (0.87)
  the two profiles are of different devices: /device:TPU:13 before, /device:TPU:0 now
where the time goes in v2:
time: 15.9 us; the launch traced here: 15.7 us
  Pallas kernels  15.1 us (95%)
  between operations  0.64 us (4%)
    pallas_call x1, Pallas kernels, on_device(): pl.pallas_call(functools.partial(kernel, n_lat, n_lon), out_shape=[vmem(p...  14.1 us
    pallas_call x1, Pallas kernels, on_device(): pl.pallas_call(functools.partial(finish, 1.0 / (rows * n_lat)), out_shape...  0.99 us

profile of v2, /device:TPU:0, one launch (start us, length us, event | category | flops | bytes accessed | tf_op | source)
XLA Modules:
  0.0 15.7 jit_solution(7553350232481444927)
XLA Ops:
  0.6 14.1 %waves.1 = (f32[32,32,128]{2,1,0:T(8,128)S(1)}, f32[32,32,128]{2,1,0:T(8,128)S(1)}, f32[32,128]{1,0:T(8,128)S(1)}) custom-call(f32[32,32,128]{2,1,0:T(8,128)} %p_in.1, f32[32,32,128]{2,1,0:T(8,128)} %e_in.1, f32[32,32,128]{2,1,0:T(8,128)} %c_in.1), custom_call_target="tpu_custom_call" | custom-call | tf_op jit(solution)/shard_map/waves/pallas_call | solution.py:271
  14.7 1.0 %finish.1 = (f32[32,32,128]{2,1,0:T(8,128)}, f32[32,32,128]{2,1,0:T(8,128)}) custom-call(f32[32,32,128]{2,1,0:T(8,128)S(1)} %get-tuple-element.5.here, f32[32,32,128]{2,1,0:T(8,128)S(1)} %get-tuple-element.6.end, f32[32,128]{1,0:T(8,128)S(1)} %get-tuple-element.7.before), custom_call_target="tpu_custom_call" | custom-call | tf_op jit(solution)/shard_map/finish/pallas_call | solution.py:292

commit v3 on v2

--- a/solution.py
+++ b/solution.py
@@ -13,7 +13,7 @@
 
 
 def corner_cells():
-    cells = [(0, i, j) for i in range(STEPS - 1) for j in range(STEPS - 1 - i)]
+    cells = [(0, i, 0) for i in range(STEPS - 1)] + [(0, 0, j) for j in range(1, STEPS - 1)]
     for array in (1, 2):
         cells += [(array, i, j) for i in range(STEPS - 2) for j in range(STEPS - 2 - i)]
     return cells
@@ -21,12 +21,15 @@
 
 def kernel(
     n_lat, n_lon, p_in, e_in, c_in, here, end, before,
-    p, e, c, lon_send, lon_recv, corner_send, corner_recv, totals, below,
-    load_sem, lat_sems, lon_sems, corner_sems, total_send_sem, total_recv_sem,
+    p, e, c, lon_send, lon_recv, corner_send, corner_recv,
+    p_recv, e_recv, c_recv, totals, below,
+    load_sem, ready_sem, lat_sems, lon_sems, corner_sems, total_send_sem, total_recv_sem,
 ):
     rows, cols = p_in.shape[0], p_in.shape[1]
     fields = (p, e, c)
-    depth = (STEPS, STEPS - 1, STEPS - 1)
+    lat_depth = (STEPS - 2, STEPS - 1, STEPS - 1)
+    lon_depth = (STEPS - 2, STEPS - 1, STEPS - 2)
+    received = (p_recv, e_recv, c_recv)
     top, left = STEPS, PAD
     bottom, right = top + rows, left + cols
     me_lat, me_lon = lax.axis_index("lat"), lax.axis_index("lon")
@@ -47,11 +50,6 @@
             barrier, inc=1, device_id={"lat": lat, "lon": lon}, device_id_type=MESH
         )
 
-    for a in range(2):
-        for b in range(2):
-            @pl.when(has_lat[a] & has_lon[b])
-            def _():
-                greet(me_lat + step_of[a], me_lon + step_of[b])
     for b in range(2):
         @pl.when(has_lon[b])
         def _():
@@ -65,8 +63,13 @@
     one = jnp.int32(1)
     count_lat = sum(jnp.where(h, one, zero) for h in has_lat)
     count_lon = sum(jnp.where(h, one, zero) for h in has_lon)
-    peers = n_lat - 1 + count_lon + count_lon * count_lat
-
+    peers = n_lat - 1 + count_lon
+
+    width = p.shape[2]
+    for r in (top - 1, bottom):
+        p[r] = jnp.zeros(p.shape[1:], p.dtype)
+    for s in (0, right):
+        p[top:bottom, s:s + PAD] = jnp.zeros((rows, PAD, width), p.dtype)
     for a in range(2):
         @pl.when(jnp.logical_not(has_lat[a]))
         def _():
@@ -83,15 +86,32 @@
     for copy in loads:
         copy.wait()
 
+    def advance(now, old, r, lo, hi):
+        middle = now[r, lo:hi]
+        spread = (
+            now[r - 1, lo:hi] + now[r + 1, lo:hi]
+            + now[r, lo - 1:hi - 1] + now[r, lo + 1:hi + 1] - 4.0 * middle
+        )
+        return 2.0 * middle - old[r, lo:hi] + c[r, lo:hi] * spread
+
+    def first_row(r, carry):
+        e[r, left:right] = advance(p, e, r, left, right)
+        return carry
+
+    lax.fori_loop(top, bottom, first_row, 0, unroll=2)
+
     for b in range(2):
         @pl.when(has_lon[b])
         def _():
             base = 0
-            for f, d in zip(fields, depth):
+            for f, d in zip(fields, lon_depth):
                 start = left if b == 0 else right - d
                 for r in range(rows):
                     lon_send[b, base + r * d:base + (r + 1) * d] = f[top + r, start:start + d]
                 base += rows * d
+            s = left + STEPS - 2 if b == 0 else right - STEPS + 1
+            for k, r in enumerate((top, bottom - 1)):
+                lon_send[b, base + k:base + k + 1] = c[r, s:s + 1]
     cells = corner_cells()
     for a in range(2):
         for b in range(2):
@@ -125,32 +145,39 @@
         )
 
     def lat_copy(a, k):
-        f, d = fields[k], depth[k]
+        f, d = fields[k], lat_depth[k]
         src = top if a == 0 else bottom - d
-        dst = bottom if a == 0 else top - d
         return pltpu.make_async_remote_copy(
             src_ref=f.at[src:src + d, left:right],
-            dst_ref=f.at[dst:dst + d, left:right],
+            dst_ref=received[k].at[1 - a],
             send_sem=lat_sems.at[0, a, k],
             recv_sem=lat_sems.at[1, 1 - a, k],
             device_id={"lat": me_lat + step_of[a], "lon": me_lon},
             device_id_type=MESH,
         )
 
+    for b in range(2):
+        @pl.when(has_lon[b])
+        def _():
+            lon_copy(b).start()
+    for a in range(2):
+        @pl.when(has_lat[a])
+        def _():
+            for k in range(3):
+                lat_copy(a, k).start()
+    for a in range(2):
+        @pl.when(has_lat[a])
+        def _():
+            pl.semaphore_signal(
+                ready_sem, inc=1, device_id={"lat": me_lat + step_of[a], "lon": me_lon},
+                device_id_type=MESH,
+            )
+    pl.semaphore_wait(ready_sem, count_lat)
     for a in range(2):
         for b in range(2):
             @pl.when(has_lat[a] & has_lon[b])
             def _():
                 corner_copy(a, b).start()
-    for b in range(2):
-        @pl.when(has_lon[b])
-        def _():
-            lon_copy(b).start()
-    for a in range(2):
-        @pl.when(has_lat[a])
-        def _():
-            for k in range(3):
-                lat_copy(a, k).start()
 
     for a in range(2):
         for b in range(2):
@@ -168,31 +195,48 @@
             lon_copy(1 - b).wait_recv()
             lon_copy(b).wait_send()
             base = 0
-            for f, d in zip(fields, depth):
+            for f, d in zip(fields, lon_depth):
                 start = left - d if b == 0 else right
                 for r in range(rows):
                     f[top + r, start:start + d] = lon_recv[b, base + r * d:base + (r + 1) * d]
                 base += rows * d
+            s = left - STEPS + 1 if b == 0 else right + STEPS - 2
+            for k, r in enumerate((top, bottom - 1)):
+                c[r, s:s + 1] = lon_recv[b, base + k:base + k + 1]
     for a in range(2):
         @pl.when(has_lat[a])
         def _():
             for k in range(3):
                 lat_copy(1 - a, k).wait_recv()
                 lat_copy(a, k).wait_send()
-
-    now, old = p, e
-    for step in range(STEPS):
+                d = lat_depth[k]
+                dst = top - d if a == 0 else bottom
+                fields[k][dst:dst + d, left:right] = received[k][a]
+
+    def add(r, lo, hi, r_from, shift):
+        e[r, lo:hi] = e[r, lo:hi] + c[r, lo:hi] * p[r_from, lo + shift:hi + shift]
+
+    for near, far in ((top, top - 1), (bottom - 1, bottom)):
+        add(near, left - 3, right + 3, far, 0)
+        add(far, left - 2, right + 2, near, 0)
+
+    def lon_edges(r, carry):
+        add(r, left, left + 1, r, -1)
+        add(r, left - 1, left, r, 1)
+        add(r, right - 1, right, r, 1)
+        add(r, right, right + 1, r, -1)
+        return carry
+
+    lax.fori_loop(top - 3, bottom + 3, lon_edges, 0, unroll=2)
+
+    now, old = e, p
+    for step in range(1, STEPS):
         margin = STEPS - 1 - step
         lo, hi = left - margin, right + margin
         last = step == STEPS - 1
 
         def one_row(r, total, now=now, old=old, lo=lo, hi=hi, last=last):
-            middle = now[r, lo:hi]
-            spread = (
-                now[r - 1, lo:hi] + now[r + 1, lo:hi]
-                + now[r, lo - 1:hi - 1] + now[r, lo + 1:hi + 1] - 4.0 * middle
-            )
-            later = 2.0 * middle - old[r, lo:hi] + c[r, lo:hi] * spread
+            later = advance(now, old, r, lo, hi)
             if not last:
                 old[r, lo:hi] = later
             else:
@@ -201,7 +245,7 @@
                 here[r - top] = total
             return total
 
-        start = jnp.zeros((cols, p.shape[2]), p.dtype) if last else 0
+        start = jnp.zeros((cols, width), p.dtype) if last else 0
         total = lax.fori_loop(top - margin, bottom + margin, one_row, start, unroll=2)
         now, old = old, now
     below[...] = total
@@ -261,7 +305,7 @@
 
 def on_device(n_lat, n_lon, pressure, earlier, speed_square):
     rows, cols, members = pressure.shape
-    packed = rows * (3 * STEPS - 2)
+    packed = -(-(rows * (3 * STEPS - 5) + 2) // 8) * 8
     corner_rows = -(-len(corner_cells()) // 8) * 8
     f32 = jnp.float32
     wide = pltpu.VMEM((rows + 2 * STEPS, cols + 2 * PAD, members), f32)
@@ -281,9 +325,12 @@
             pltpu.VMEM((2, packed, members), f32),
             pltpu.VMEM((4, corner_rows, members), f32),
             pltpu.VMEM((4, corner_rows, members), f32),
+            pltpu.VMEM((2, STEPS - 2, cols, members), f32),
+            pltpu.VMEM((2, STEPS - 1, cols, members), f32),
+            pltpu.VMEM((2, STEPS - 1, cols, members), f32),
             pltpu.VMEM((n_lat, cols, members), f32),
             pltpu.VMEM((cols, members), f32),
-            dma((3,)), dma((2, 2, 3)), dma((2, 2)), dma((2, 4)),
+            dma((3,)), pltpu.SemaphoreType.REGULAR, dma((2, 2, 3)), dma((2, 2)), dma((2, 4)),
             dma((n_lat,)), dma((n_lat,)),
         ],
         compiler_params=pltpu.CompilerParams(collective_id=0, has_side_effects=True),

time: 15.9 us -> 14.6 us (0.918)
  Pallas kernels: 15.1 us -> 13.9 us
    pallas_call x1, Pallas kernels: 14.1 us -> 12.9 us  [on_device(): pl.pallas_call(functools.partial(kernel, n_lat, n_lon), out_shape=[vmem(p...]
where the time goes in v3:
time: 14.6 us; the launch traced here: 14.5 us
  Pallas kernels  13.9 us (95%)
  between operations  0.64 us (4%)
    pallas_call x1, Pallas kernels, on_device(): pl.pallas_call(functools.partial(kernel, n_lat, n_lon), out_shape=[vmem(p...  12.9 us
    pallas_call x1, Pallas kernels, on_device(): pl.pallas_call(functools.partial(finish, 1.0 / (rows * n_lat)), out_shape...  0.99 us

profile of v3, /device:TPU:0, one launch (start us, length us, event | category | flops | bytes accessed | tf_op | source)
XLA Modules:
  0.0 14.5 jit_solution(2238788593462665047)
XLA Ops:
  0.6 12.9 %waves.1 = (f32[32,32,128]{2,1,0:T(8,128)S(1)}, f32[32,32,128]{2,1,0:T(8,128)S(1)}, f32[32,128]{1,0:T(8,128)S(1)}) custom-call(f32[32,32,128]{2,1,0:T(8,128)} %p_in.1, f32[32,32,128]{2,1,0:T(8,128)} %e_in.1, f32[32,32,128]{2,1,0:T(8,128)} %c_in.1), custom_call_target="tpu_custom_call" | custom-call | tf_op jit(solution)/shard_map/waves/pallas_call | solution.py:315
  13.5 1.0 %finish.1 = (f32[32,32,128]{2,1,0:T(8,128)}, f32[32,32,128]{2,1,0:T(8,128)}) custom-call(f32[32,32,128]{2,1,0:T(8,128)S(1)} %get-tuple-element.5.here, f32[32,32,128]{2,1,0:T(8,128)S(1)} %get-tuple-element.6.end, f32[32,128]{1,0:T(8,128)S(1)} %get-tuple-element.7.before), custom_call_target="tpu_custom_call" | custom-call | tf_op jit(solution)/shard_map/finish/pallas_call | solution.py:339

commit v4 on v3

--- a/solution.py
+++ b/solution.py
@@ -98,7 +98,7 @@
         e[r, left:right] = advance(p, e, r, left, right)
         return carry
 
-    lax.fori_loop(top, bottom, first_row, 0, unroll=2)
+    lax.fori_loop(top, bottom, first_row, 0, unroll=4)
 
     for b in range(2):
         @pl.when(has_lon[b])
@@ -179,6 +179,26 @@
             def _():
                 corner_copy(a, b).start()
 
+    unroll = 4
+
+    def put(now, old, r, lo, hi, last):
+        later = advance(now, old, r, lo, hi)
+        if last:
+            end[r - top, lo - left:hi - left] = later
+        else:
+            old[r, lo:hi] = later
+
+    now, old = e, p
+    for step in range(1, STEPS):
+        inside = step + 1
+
+        def inner_row(r, carry, now=now, old=old, inside=inside, last=step == STEPS - 1):
+            put(now, old, r, left + inside, right - inside, last)
+            return carry
+
+        lax.fori_loop(top + inside, bottom - inside, inner_row, 0, unroll=unroll)
+        now, old = old, now
+
     for a in range(2):
         for b in range(2):
             @pl.when(has_lat[a] & has_lon[b])
@@ -189,6 +209,16 @@
                     r = top - 1 - i if a == 0 else bottom + i
                     s = left - 1 - j if b == 0 else right + j
                     fields[which][r, s:s + 1] = corner_recv[2 * a + b, k:k + 1]
+    for a in range(2):
+        @pl.when(has_lat[a])
+        def _():
+            for k in range(3):
+                lat_copy(1 - a, k).wait_recv()
+                lat_copy(a, k).wait_send()
+                d = lat_depth[k]
+                dst = top - d if a == 0 else bottom
+                fields[k][dst:dst + d, left:right] = received[k][a]
+
     for b in range(2):
         @pl.when(has_lon[b])
         def _():
@@ -203,15 +233,6 @@
             s = left - STEPS + 1 if b == 0 else right + STEPS - 2
             for k, r in enumerate((top, bottom - 1)):
                 c[r, s:s + 1] = lon_recv[b, base + k:base + k + 1]
-    for a in range(2):
-        @pl.when(has_lat[a])
-        def _():
-            for k in range(3):
-                lat_copy(1 - a, k).wait_recv()
-                lat_copy(a, k).wait_send()
-                d = lat_depth[k]
-                dst = top - d if a == 0 else bottom
-                fields[k][dst:dst + d, left:right] = received[k][a]
 
     def add(r, lo, hi, r_from, shift):
         e[r, lo:hi] = e[r, lo:hi] + c[r, lo:hi] * p[r_from, lo + shift:hi + shift]
@@ -231,23 +252,24 @@
 
     now, old = e, p
     for step in range(1, STEPS):
-        margin = STEPS - 1 - step
+        margin, inside, last = STEPS - 1 - step, step + 1, step == STEPS - 1
         lo, hi = left - margin, right + margin
-        last = step == STEPS - 1
-
-        def one_row(r, total, now=now, old=old, lo=lo, hi=hi, last=last):
-            later = advance(now, old, r, lo, hi)
-            if not last:
-                old[r, lo:hi] = later
-            else:
-                end[r - top] = later
-                total = total + later
-                here[r - top] = total
-            return total
-
-        start = jnp.zeros((cols, width), p.dtype) if last else 0
-        total = lax.fori_loop(top - margin, bottom + margin, one_row, start, unroll=2)
+        for r in list(range(top - margin, top + inside)) + list(
+            range(bottom - inside, bottom + margin)
+        ):
+            put(now, old, r, lo, hi, last)
+
+        def side_row(r, carry, now=now, old=old, lo=lo, hi=hi, inside=inside, last=last):
+            put(now, old, r, lo, left + inside, last)
+            put(now, old, r, right - inside, hi, last)
+            return carry
+
+        lax.fori_loop(top + inside, bottom - inside, side_row, 0, unroll=unroll)
         now, old = old, now
+    parts = [end[r] for r in range(4)]
+    for r in range(4, rows):
+        parts[r % 4] = parts[r % 4] + end[r]
+    total = (parts[0] + parts[1]) + (parts[2] + parts[3])
     below[...] = total
 
     def total_copy(j):
@@ -274,6 +296,13 @@
         @pl.when(me_lat < j)
         def _():
             total_copy(j).start()
+    def sum_row(r, running):
+        running = running + end[r]
+        here[r] = running
+        return running
+
+    lax.fori_loop(0, rows, sum_row, jnp.zeros((cols, width), p.dtype), unroll=4)
+
     def arrive(j, acc):
         total_arrival(j).wait_recv()
         return acc + totals[j]

time: 14.6 us -> 14.2 us (0.973)
  Pallas kernels: 13.9 us -> 13.5 us
    pallas_call x1, Pallas kernels: 12.9 us -> 12.5 us  [on_device(): pl.pallas_call(functools.partial(kernel, n_lat, n_lon), out_shape=[vmem(p...]
where the time goes in v4:
time: 14.2 us; the launch traced here: 14.1 us
  Pallas kernels  13.5 us (95%)
  between operations  0.64 us (5%)
    pallas_call x1, Pallas kernels, on_device(): pl.pallas_call(functools.partial(kernel, n_lat, n_lon), out_shape=[vmem(p...  12.5 us
    pallas_call x1, Pallas kernels, on_device(): pl.pallas_call(functools.partial(finish, 1.0 / (rows * n_lat)), out_shape...  0.99 us

profile of v4, /device:TPU:0, one launch (start us, length us, event | category | flops | bytes accessed | tf_op | source)
XLA Modules:
  0.0 14.1 jit_solution(7460523858030116432)
XLA Ops:
  0.6 12.5 %waves.1 = (f32[32,32,128]{2,1,0:T(8,128)S(1)}, f32[32,32,128]{2,1,0:T(8,128)S(1)}, f32[32,128]{1,0:T(8,128)S(1)}) custom-call(f32[32,32,128]{2,1,0:T(8,128)} %p_in.1, f32[32,32,128]{2,1,0:T(8,128)} %e_in.1, f32[32,32,128]{2,1,0:T(8,128)} %c_in.1), custom_call_target="tpu_custom_call" | custom-call | tf_op jit(solution)/shard_map/waves/pallas_call | solution.py:344
  13.1 1.0 %finish.1 = (f32[32,32,128]{2,1,0:T(8,128)}, f32[32,32,128]{2,1,0:T(8,128)}) custom-call(f32[32,32,128]{2,1,0:T(8,128)S(1)} %get-tuple-element.5.here, f32[32,32,128]{2,1,0:T(8,128)S(1)} %get-tuple-element.6.end, f32[32,128]{1,0:T(8,128)S(1)} %get-tuple-element.7.before), custom_call_target="tpu_custom_call" | custom-call | tf_op jit(solution)/shard_map/finish/pallas_call | solution.py:368
